TPU v7x, 256 devices: a whole 4x4x8 slice. The times are simulated.
256 devices in a mesh: tower: 2 (over x_lo), blk: 128 (over z, y, x_hi, core).
Axes of the slice: x: 4 (x_hi: 2, x_lo: 2; x = x_hi * 2 + x_lo), y: 4, z: 8, core: 2. Of those that a mesh axis runs over, the one named last changes fastest.
Arguments:
- pooled: bfloat16 [2, 16384, 1152], P('tower', 'blk'), may hold values from -6 to 6
- final_gain: float32 [2, 1152], P('tower'), may hold values from 0.5 to 1.5
- head_weight: bfloat16 [2, 1152, 1152], P('tower'), may hold values from -0.1875 to 0.1875
- pair_ids: int32 [16384], replicated, may hold values from 0 to 16383
- log_scale: float32 [1], replicated, may hold values from 4.2 to 4.7
- bias: float32 [1], replicated, may hold values from -4 to -1
Outputs:
- emb_grad: float32 [2, 16384, 1152], P('tower', 'blk')
Inputs may be any that keep to these rules, and one draw needn't show every extreme that they name: `pair_ids`: examples with equal ids form positive pairs; every example is a positive pair with its own image and text.
All inputs are finite; a program needn't handle non-finite values.
Results may differ from a plain program's by a relative error of at most 0.0043.
Values may be sent and summed in bfloat16 or wider, within the bound.
No kernel may reach another device: no remote copies, remote signals or barrier semaphores. Data moves between devices by JAX's collectives and lax.ppermute only.
A program may use at most 192 MiB of HBM per device.

v0:
```python
import jax
import jax.numpy as jnp
from jax import lax
from jax.sharding import PartitionSpec as P


def partner(value, axis, stride):
    mask = 2**stride
    pairs = [(source, source ^ mask) for source in range(lax.axis_size(axis))]
    return lax.ppermute(value, axis, pairs)


def embed_rows(feats, gain, weight):
    values = feats.astype(jnp.float32)
    center = values - jnp.mean(values, axis=-1, keepdims=True)
    spread = jnp.mean(center * center, axis=-1, keepdims=True)
    normed = (center * lax.rsqrt(spread + 1e-06) * gain).astype(jnp.bfloat16)
    head = jnp.dot(normed, weight, preferred_element_type=jnp.float32)
    length = jnp.sum(head * head, axis=-1, keepdims=True)
    return (head * lax.rsqrt(length + 1e-06)).astype(jnp.bfloat16)


def pair_coef(fixed_rows, moving_rows, fixed_ids, moving_ids, scale, shift):
    logits = (
        scale
        * lax.dot_general(
            fixed_rows, moving_rows, (((1,), (1,)), ((), ())), preferred_element_type=jnp.float32
        )
        + shift
    )
    sign = jnp.where(fixed_ids[:, None] == moving_ids[None, :], jnp.float32(1.0), jnp.float32(-1.0))
    return (-sign * jax.nn.sigmoid(-sign * logits)).astype(jnp.bfloat16)


def pair_forces(fixed_rows, moving_rows, fixed_ids, moving_ids, scale, shift):
    coef = pair_coef(fixed_rows, moving_rows, fixed_ids, moving_ids, scale, shift)
    return jnp.dot(coef, moving_rows, preferred_element_type=jnp.float32)


def on_device(pooled, final_gain, head_weight, pair_ids, log_scale, bias):
    local_embed = embed_rows(pooled[0], final_gain[0], head_weight[0])
    count = local_embed.shape[0]
    scale = jnp.exp(log_scale[0])
    shift = bias[0]
    block_index = lax.axis_index("blk")
    local_ids = lax.dynamic_slice_in_dim(pair_ids, block_index * count, count)
    partner_embed = partner(local_embed, "tower", 0)
    total = pair_forces(
        local_embed,
        lax.all_gather(partner_embed, "blk", axis=0, tiled=True),
        local_ids,
        pair_ids,
        scale,
        shift,
    )
    return total[None]


def solution(mesh):
    placed = (P("tower", "blk", None), P("tower", None), P("tower", None, None), P(), P(), P())
    return jax.shard_map(
        on_device, mesh=mesh, in_specs=placed, out_specs=P("tower", "blk", None), check_vma=False
    )
```

profile of v0, /device:TPU:1, one launch (start us, length us, event | category | flops | bytes accessed | tf_op | source)
XLA Modules:
  0.0 296.5 jit_solution(8610071853615321268)
XLA Ops:
  6.5 0.0 copy-start
  6.5 0.0 all-gather.2.cloned.1.call-start
  6.5 1.2 convert_reduce_fusion
  7.8 1.2 fusion.23
  9.0 0.7 reduce.1
  9.7 0.0 copy-done
  9.7 1.7 multiply_reduce_fusion
  11.4 0.1 multiply_convert_fusion
  11.5 2.1 collective-permute-start
  13.7 5.5 %collective-permute-done = bf16[128,1152]{1,0:T(8,128)(2,1)S(1)} collective-permute-done((bf16[128,1152]{1,0:T(8,128)(2,1)S(1)}, bf16[128,1152]{1,0:T(8,128)(2,1)S(1)}, u32[]{:S(2)}, u32[]{:S(2)}) %collective-permute-start) | collective-permute-done | bytes 294944 | tf_op jit(solution)/shard_map/ppermute | solution.py:10
  19.1 0.0 copy-start.1
  19.1 0.7 copy-done.1
  19.8 0.0 all-gather.2.cloned.1.call-update
  21.2 0.8 dynamic_slice.3
  22.0 231.2 %all-gather.2.cloned.1.call-done = bf16[16384,1152]{1,0:T(8,128)(2,1)} async-done(((bf16[128,1152]{1,0:T(8,128)(2,1)}), bf16[16384,1152]{1,0:T(8,128)(2,1)}) %all-gather.2.cloned.1.call-update) | async-done | bytes 37748752 | tf_op jit(solution)/shard_map/all_gather | solution.py:50
  253.2 36.4 %fusion.17 = f32[1,128,1152]{2,1,0:T(8,128)} fusion(bf16[16384,1152]{1,0:T(8,128)(2,1)} %all-gather.2.cloned.1.call-done, bf16[128,1152]{1,0:T(8,128)(2,1)S(1)} %multiply_convert_fusion, f32[]{:T(128)} %bitcast.25, f32[]{:T(128)} %bitcast, s32[16384]{0:T(1024)} %param.9, s32[128]{0:T(128)S(1)} %dynamic_slice.3), kind=kOutput, calls=%fused_computation.18 | convolution fusion | flops 9686745088 | bytes 38699528 | tf_op jit(solution)/shard_map/dot_general | solution.py:37
  (3 shorter events, 0.0 us)
Async XLA Ops:
  6.5 3.2 %copy-start = (bf16[1,1152,1152]{2,1,0:T(8,128)(2,1)S(1)}, bf16[1,1152,1152]{2,1,0:T(8,128)(2,1)}, u32[]{:S(2)}) copy-start(bf16[1,1152,1152]{2,1,0:T(8,128)(2,1)} %param.8) | copy-start | bytes 7962628
  6.5 246.7 %all-gather.2.cloned.1.call-start = ((), (), s32[]{:S(2)}) async-start(), calls=%async_computation | async-start | bytes 38043648 | tf_op jit(solution)/shard_map/all_gather | solution.py:50
  11.5 7.6 %collective-permute-start = (bf16[128,1152]{1,0:T(8,128)(2,1)S(1)}, bf16[128,1152]{1,0:T(8,128)(2,1)S(1)}, u32[]{:S(2)}, u32[]{:S(2)}) collective-permute-start(bf16[128,1152]{1,0:T(8,128)(2,1)S(1)} %multiply_convert_fusion), channel_id=1, source_target_pairs={{0,128},{128,0},{1,129},{129,1},{2,130},{130,2},{3,131},{131,3},{4... | collective-permute-start | bytes 884744 | tf_op jit(solution)/shard_map/ppermute | solution.py:10
  19.1 0.7 copy-start.1
Sparse Core Ops, SparseCore 0:
  20.0 233.1 all-gather.1
where the time goes:
time: 297 us; the launch traced here: 296 us
  waiting for transfers between devices  237 us (80%)
  matrix products  38.1 us (13%)
  between operations  14.8 us (5%)
  other arithmetic  3.27 us (1%)
    all_gather x1, waiting for transfers between devices, on_device(): lax.all_gather(partner_embed, 'blk', axis=0, tiled=True)  231 us
    dot_general x1, matrix products, pair_forces(): return jnp.dot(coef, moving_rows, preferred_element_type=jnp.float32)  36.4 us
  transfers between devices with their start and end apart: 2, of which 2 were waited for; matrix products, arithmetic and copies ran while one was open for 0% of the time, Pallas kernels for 0%

commit v1 on v0

v1 whole, which is shorter than its diff:
```python
import jax
import jax.numpy as jnp
from jax import lax
from jax.sharding import PartitionSpec as P

NZ, NY, NH, NC = 8, 4, 2, 2
BLK = NZ * NY * NH * NC


def hop(value, route):
    pairs = []
    for m in range(2):
        for b in range(BLK):
            c, h, y, z = b % NC, b // NC % NH, b // (NC * NH) % NY, b // (NC * NH * NY)
            goal = route(m, z, y, h, c)
            if goal is None:
                continue
            tm, tz, ty, th, tc = goal
            target = ((tz % NZ * NY + ty % NY) * NH + th) * NC + tc
            pairs.append((m * BLK + b, tm * BLK + target))
    return lax.ppermute(value, ("tower", "blk"), pairs)


def embed_rows(feats, gain, weight):
    values = feats.astype(jnp.float32)
    center = values - jnp.mean(values, axis=-1, keepdims=True)
    spread = jnp.mean(center * center, axis=-1, keepdims=True)
    normed = (center * lax.rsqrt(spread + 1e-06) * gain).astype(jnp.bfloat16)
    head = jnp.dot(normed, weight, preferred_element_type=jnp.float32)
    length = jnp.sum(head * head, axis=-1, keepdims=True)
    return (head * lax.rsqrt(length + 1e-06)).astype(jnp.bfloat16)


def pair_coef(image_rows, text_rows, image_ids, text_ids, scale, shift):
    logits = (
        scale
        * lax.dot_general(
            image_rows, text_rows, (((1,), (1,)), ((), ())), preferred_element_type=jnp.float32
        )
        + shift
    )
    match = image_ids[:, None] == text_ids[None, :]
    share = jax.nn.sigmoid(jnp.where(match, -logits, logits))
    return jnp.where(match, -share, share).astype(jnp.bfloat16)


def on_device(pooled, final_gain, head_weight, pair_ids, log_scale, bias):
    bf16, f32 = jnp.bfloat16, jnp.float32
    local = embed_rows(pooled[0], final_gain[0], head_weight[0])
    ex = local.shape[0]
    half = ex // 2
    scale = jnp.exp(log_scale[0])
    shift = bias[0]
    m = lax.axis_index("tower")
    b = lax.axis_index("blk")
    c, h, y, z = b % NC, b // NC % NH, b // (NC * NH) % NY, b // (NC * NH * NY)
    first = c == 0
    image_side = m == 0

    p1 = hop(local, lambda m, z, y, h, c: (0, z, y, h, c) if m else ((1, z, y, h, 1) if c else None))
    p2 = hop(local, lambda m, z, y, h, c: (0, z, y, 1 - h, c) if m else ((1, z, y, h, 0) if c else None))
    p3 = hop(local, lambda m, z, y, h, c: (1, z, y, 1 - h, c) if m else (None if c else (0, z, y, h, 1)))
    text_own = jnp.where(image_side, p1, local)
    text_oth = jnp.where(image_side, p2, p3)
    image = jnp.where(image_side, jnp.where(first, local, p3), jnp.where(first, p2, p1))

    up_y = lambda m, z, y, h, c: (m, z, y + 1, h, c)
    down_y = lambda m, z, y, h, c: (m, z, y - 1, h, c)
    below = [hop(text_own, up_y), hop(text_oth, up_y)]
    above = [hop(text_own, down_y), hop(text_oth, down_y)]
    far = [hop(below[0], up_y), hop(above[1], down_y)]
    texts = [text_own, text_oth] + below + above + far

    ring = lambda m, z, y, h, c: (m, z - 1 if c else z + 1, y, h, c)
    unring = lambda m, z, y, h, c: (m, z + 1 if c else z - 1, y, h, c)
    swap = lambda m, z, y, h, c: (m, z, y, h, 1 - c)
    got, images = image, [image]
    for _ in range(NZ // 2 - 1):
        got = hop(got, ring)
        images += [got, hop(got, swap)]
    last = hop(jnp.where(first, got[:half], got[half:]), ring)
    last_oth = hop(last, swap)
    images.append(
        jnp.where(first, jnp.concatenate([last, last_oth]), jnp.concatenate([last_oth, last]))
    )

    ids = pair_ids.reshape(NZ, NY, NH, NC, ex)
    image_col = lax.dynamic_slice(ids, (0, y, h, m, 0), (NZ, 1, 1, 1, ex)).reshape(NZ, ex)
    step = jnp.where(first, -1, 1)
    image_order = [0] + [s for k in range(1, NZ // 2) for s in (k, -k)] + [NZ // 2]
    image_ids = jnp.concatenate(
        [lax.dynamic_slice_in_dim(image_col, (z + step * k) % NZ, 1)[0] for k in image_order]
    )
    text_col = lax.dynamic_slice(ids, (z, 0, 0, c, 0), (1, NY, NH, 1, ex)).reshape(NY * NH, ex)
    text_order = [(0, 0), (0, 1), (-1, 0), (-1, 1), (1, 0), (1, 1), (2, 0), (2, 1)]
    text_ids = jnp.concatenate(
        [
            lax.dynamic_slice_in_dim(text_col, (y + dy) % NY * NH + (h if dh == 0 else 1 - h), 1)[0]
            for dy, dh in text_order
        ]
    )

    image_rows = jnp.concatenate(images)
    text_rows = jnp.concatenate(texts)
    coef = pair_coef(image_rows, text_rows, image_ids, text_ids, scale, shift)
    image_part = jnp.dot(coef, text_rows, preferred_element_type=f32)
    text_part = lax.dot_general(
        coef, image_rows, (((0,), (0,)), ((), ())), preferred_element_type=f32
    )

    part = [text_part[k * ex : (k + 1) * ex] for k in range(NY * NH)]
    part[4] = part[4] + hop(part[6].astype(bf16), up_y)
    part[3] = part[3] + hop(part[7].astype(bf16), down_y)
    own, oth = (
        part[k] + hop(part[k + 4].astype(bf16), up_y) + hop(part[k + 2].astype(bf16), down_y)
        for k in range(2)
    )
    own_send, oth_send = own.astype(bf16), oth.astype(bf16)
    text_grad = (
        own
        + hop(own_send, lambda m, z, y, h, c: None if m else (1, z, y, h, c))
        + hop(oth_send, lambda m, z, y, h, c: None if m else (1, z, y, 1 - h, c))
        + hop(oth_send, lambda m, z, y, h, c: (1, z, y, 1 - h, c) if m else None)
    )

    slab = [image_part[k * ex : (k + 1) * ex] for k in range(NZ)]
    end = slab[-1].astype(bf16)
    give = jnp.concatenate(
        [s.astype(bf16) for s in slab[2:7:2]] + [jnp.where(first, end[half:], end[:half])]
    )
    take = hop(give, swap)
    acc = jnp.where(first, slab[-1][:half], slab[-1][half:]) + take[-half:]
    came = hop(acc.astype(bf16), unring).astype(f32)
    pad = jnp.zeros_like(came)
    came = jnp.where(first, jnp.concatenate([came, pad]), jnp.concatenate([pad, came]))
    for k in (2, 1, 0):
        acc = slab[1 + 2 * k] + take[k * ex : (k + 1) * ex] + came
        came = hop(acc.astype(bf16), unring).astype(f32)
    mine = slab[0] + came
    mine_send = mine.astype(bf16)
    fa = hop(mine_send, lambda m, z, y, h, c: (0, z, y, h, m) if c else None)
    fb = hop(mine_send, lambda m, z, y, h, c: (0, z, y, h, 1) if m and not c else None)
    image_grad = jnp.where(first, mine, fb) + fa

    return jnp.where(image_side, image_grad, text_grad)[None]


def solution(mesh):
    placed = (P("tower", "blk", None), P("tower", None), P("tower", None, None), P(), P(), P())
    return jax.shard_map(
        on_device, mesh=mesh, in_specs=placed, out_specs=P("tower", "blk", None), check_vma=False
    )
```

time: 297 us -> 130 us (0.44)
  waiting for transfers between devices: 237 us -> 41.2 us
  starting transfers between devices: 2.12 us -> 59.6 us
  matrix products: 38.1 us -> 11.6 us
  between operations: 14.8 us -> 2.23 us
  local copies, waits for them, and re-layouts: 1.48 us -> 6.85 us
  other arithmetic: 3.27 us -> 7.61 us
    all_gather x1 -> x0, waiting for transfers between devices: 231 us -> none  [on_device(): lax.all_gather(partner_embed, 'blk', axis=0, tiled=True)]
    ppermute x1 -> x33, starting transfers between devices: 2.12 us -> 59.6 us  [hop(): return lax.ppermute(value, ('tower', 'blk'), pairs)]
    ppermute x1 -> x33, waiting for transfers between devices: 5.47 us -> 41.2 us  [hop(): return lax.ppermute(value, ('tower', 'blk'), pairs)]
    dot_general x1 -> x3, matrix products: 36.4 us -> 9.94 us  [the longest x1 4.09 us: pair_coef(): lax.dot_general(image_rows, text_rows, (((1,), (1,)), ((), ())), preferre...]
    unnamed x4 -> x27, local copies, waits for them, and re-layouts: 0.72 us -> 5.26 us
  transfers between devices with their start and end apart: 2 -> 33, of which waited for: 2 -> 14; matrix products, arithmetic and copies ran while one was open for 0% -> 9% of each run, Pallas kernels for 0% -> 0%
where the time goes in v1:
time: 130 us; the launch traced here: 129 us
  starting transfers between devices  59.6 us (46%)
  waiting for transfers between devices  41.2 us (32%)
  matrix products  11.6 us (9%)
  other arithmetic  7.61 us (6%)
  local copies, waits for them, and re-layouts  6.85 us (5%)
  between operations  2.23 us (2%)
    ppermute x33, starting transfers between devices, hop(): return lax.ppermute(value, ('tower', 'blk'), pairs)  59.6 us
    ppermute x33, waiting for transfers between devices, hop(): return lax.ppermute(value, ('tower', 'blk'), pairs)  41.2 us
    unnamed x27, local copies, waits for them, and re-layouts  5.26 us
    dot_general x1, matrix products, pair_coef(): lax.dot_general(image_rows, text_rows, (((1,), (1,)), ((), ())), preferre...  4.09 us
    dot_general x1, matrix products, on_device(): lax.dot_general(coef, image_rows, (((0,), (0,)), ((), ())), preferred_ele...  2.97 us
    dot_general x1, matrix products, on_device(): image_part = jnp.dot(coef, text_rows, preferred_element_type=f32)  2.88 us
  transfers between devices with their start and end apart: 33, of which 14 were waited for; matrix products, arithmetic and copies ran while one was open for 9% of the time, Pallas kernels for 0%

profile of v1, /device:TPU:1, one launch (start us, length us, event | category | flops | bytes accessed | tf_op | source)
XLA Modules:
  0.0 129.1 jit_solution(1332382692783015283)
XLA Ops:
  0.0 1.2 convert_reduce_fusion
  1.2 1.2 fusion.12
  2.4 0.7 reduce.1
  3.2 1.7 %multiply_reduce_fusion = (f32[128]{0:T(128)S(1)}, f32[128,1152]{1,0:T(8,128)S(1)}) fusion(bf16[1,1152,1152]{2,1,0:T(8,128)(2,1)S(1)} %copy-done, bf16[1,128,1152]{2,1,0:T(8,128)(2,1)} %param.6, f32[1152]{0:T(1024)S(1)} %reduce.1, f32[128]{0:T(128)S(1)} %add_rsqrt_fusion.1, f32[128]{0:T(128)S(1)} %broadcast_multiply_fusion), kind=kOutput, calls=%fused_computation.40 | convolution fusion | flops 340770688 | bytes 3545088 | tf_op jit(solution)/shard_map/dot_general | solution.py:29
  4.9 0.8 multiply_convert_fusion
  5.7 3.9 %collective-permute-start.2 = (bf16[128,1152]{1,0:T(8,128)(2,1)}, bf16[128,1152]{1,0:T(8,128)(2,1)S(1)}, u32[]{:S(2)}, u32[]{:S(2)}) collective-permute-start(bf16[128,1152]{1,0:T(8,128)(2,1)} %multiply_convert_fusion), channel_id=1, source_target_pairs={{1,129},{3,131},{5,133},{7,135},{9,137},{11,139},{13,141},{15,143}... | collective-permute-start | bytes 884744 | tf_op jit(solution)/shard_map/ppermute | solution.py:21
  9.6 1.3 %collective-permute-start = (bf16[128,1152]{1,0:T(8,128)(2,1)}, bf16[128,1152]{1,0:T(8,128)(2,1)}, u32[]{:S(2)}, u32[]{:S(2)}) collective-permute-start(bf16[128,1152]{1,0:T(8,128)(2,1)} %multiply_convert_fusion), channel_id=1, source_target_pairs={{0,1},{2,3},{4,5},{6,7},{8,9},{10,11},{12,13},{14,15},{16,17},{18,... | collective-permute-start | bytes 884744 | tf_op jit(solution)/shard_map/ppermute | solution.py:21
  10.9 6.1 %collective-permute-start.1 = (bf16[128,1152]{1,0:T(8,128)(2,1)}, bf16[128,1152]{1,0:T(8,128)(2,1)}, u32[]{:S(2)}, u32[]{:S(2)}) collective-permute-start(bf16[128,1152]{1,0:T(8,128)(2,1)} %multiply_convert_fusion), channel_id=1, source_target_pairs={{1,128},{3,130},{5,132},{7,134},{9,136},{11,138},{13,140},{15,142}... | collective-permute-start | bytes 884744 | tf_op jit(solution)/shard_map/ppermute | solution.py:21
  18.8 0.7 constant_dynamic-update-slice_fusion
  19.5 0.7 constant_dynamic-update-slice_fusion.29
  20.2 0.7 constant_dynamic-update-slice_fusion.27
  20.9 0.7 constant_dynamic-update-slice_fusion.25
  21.6 0.7 constant_dynamic-update-slice_fusion.23
  22.3 0.7 constant_dynamic-update-slice_fusion.21
  22.9 0.7 constant_dynamic-update-slice_fusion.19
  23.6 0.7 constant_dynamic-update-slice_fusion.17
  24.3 0.7 constant_dynamic-slice_fusion.8
  25.2 0.1 constant_dynamic-update-slice_fusion.16
  25.3 1.4 %collective-permute-start.11 = (bf16[128,1152]{1,0:T(8,128)(2,1)S(1)}, bf16[128,1152]{1,0:T(8,128)(2,1)S(1)}, u32[]{:S(2)}, u32[]{:S(2)}) collective-permute-start(bf16[128,1152]{1,0:T(8,128)(2,1)S(1)} %get-tuple-element.8), channel_id=1, source_target_pairs={{0,4},{1,5},{2,6},{3,7},{4,8},{5,9},{6,10},{7,11},{8,12},{9,13},{1... | collective-permute-start | bytes 884744 | tf_op jit(solution)/shard_map/ppermute | solution.py:21
  26.7 1.3 %constant_dynamic-update-slice_fusion.15 = (bf16[1024,1152]{1,0:T(8,128)(2,1)S(1)}, bf16[128,1152]{1,0:T(8,128)(2,1)S(1)}, bf16[1024,1152]{1,0:T(8,128)(2,1)S(1)}, bf16[128,1152]{1,0:T(8,128)(2,1)S(1)}) fusion(bf16[1024,1152]{1,0:T(8,128)(2,1)S(1)} %get-tuple-element.7, bf16[128,1152]{1,0:T(8,128)(2,1)} %collective-permute-done.1, ...), kind=kLoop, calls=%fused_computation.72 | loop fusion | flops 884735 | bytes 2654722
  28.0 1.4 %collective-permute-start.12 = (bf16[128,1152]{1,0:T(8,128)(2,1)S(1)}, bf16[128,1152]{1,0:T(8,128)(2,1)S(1)}, u32[]{:S(2)}, u32[]{:S(2)}) collective-permute-start(bf16[128,1152]{1,0:T(8,128)(2,1)S(1)} %get-tuple-element.6), channel_id=1, source_target_pairs={{0,4},{1,5},{2,6},{3,7},{4,8},{5,9},{6,10},{7,11},{8,12},{9,13},{1... | collective-permute-start | bytes 884744 | tf_op jit(solution)/shard_map/ppermute | solution.py:21
  29.4 1.4 %collective-permute-start.14 = (bf16[128,1152]{1,0:T(8,128)(2,1)S(1)}, bf16[128,1152]{1,0:T(8,128)(2,1)S(1)}, u32[]{:S(2)}, u32[]{:S(2)}) collective-permute-start(bf16[128,1152]{1,0:T(8,128)(2,1)S(1)} %get-tuple-element.6), channel_id=1, source_target_pairs={{0,12},{1,13},{2,14},{3,15},{4,0},{5,1},{6,2},{7,3},{8,4},{9,5},{1... | collective-permute-start | bytes 884744 | tf_op jit(solution)/shard_map/ppermute | solution.py:21
  30.8 5.6 %collective-permute-start.3 = (bf16[128,1152]{1,0:T(8,128)(2,1)S(1)}, bf16[128,1152]{1,0:T(8,128)(2,1)S(1)}, u32[]{:S(2)}, u32[]{:S(2)}) collective-permute-start(bf16[128,1152]{1,0:T(8,128)(2,1)S(1)} %get-tuple-element.21), channel_id=1, source_target_pairs={{0,16},{1,113},{2,18},{3,115},{4,20},{5,117},{6,22},{7,119},{8,24}... | collective-permute-start | bytes 884744 | tf_op jit(solution)/shard_map/ppermute | solution.py:21
  36.3 0.3 collective-permute-start.13
  36.7 1.1 collective-permute-start.15
  37.8 2.2 %collective-permute-done.3 = bf16[128,1152]{1,0:T(8,128)(2,1)S(1)} collective-permute-done((bf16[128,1152]{1,0:T(8,128)(2,1)S(1)}, bf16[128,1152]{1,0:T(8,128)(2,1)S(1)}, u32[]{:S(2)}, u32[]{:S(2)}) %collective-permute-start.3) | collective-permute-done | bytes 294944 | tf_op jit(solution)/shard_map/ppermute | solution.py:21
  40.0 2.0 %collective-permute-done.12 = bf16[128,1152]{1,0:T(8,128)(2,1)S(1)} collective-permute-done((bf16[128,1152]{1,0:T(8,128)(2,1)S(1)}, bf16[128,1152]{1,0:T(8,128)(2,1)S(1)}, u32[]{:S(2)}, u32[]{:S(2)}) %collective-permute-start.12) | collective-permute-done | bytes 294944 | tf_op jit(solution)/shard_map/ppermute | solution.py:21
  42.0 5.6 %collective-permute-start.5 = (bf16[128,1152]{1,0:T(8,128)(2,1)S(1)}, bf16[128,1152]{1,0:T(8,128)(2,1)S(1)}, u32[]{:S(2)}, u32[]{:S(2)}) collective-permute-start(bf16[128,1152]{1,0:T(8,128)(2,1)S(1)} %collective-permute-done.3), channel_id=1, source_target_pairs={{0,16},{1,113},{2,18},{3,115},{4,20},{5,117},{6,22},{7,119},{8,24}... | collective-permute-start | bytes 884744 | tf_op jit(solution)/shard_map/ppermute | solution.py:21
  47.6 1.5 %collective-permute-start.16 = (bf16[128,1152]{1,0:T(8,128)(2,1)S(1)}, bf16[128,1152]{1,0:T(8,128)(2,1)S(1)}, u32[]{:S(2)}, u32[]{:S(2)}) collective-permute-start(bf16[128,1152]{1,0:T(8,128)(2,1)S(1)} %collective-permute-done.14), channel_id=1, source_target_pairs={{0,12},{1,13},{2,14},{3,15},{4,0},{5,1},{6,2},{7,3},{8,4},{9,5},{1... | collective-permute-start | bytes 884744 | tf_op jit(solution)/shard_map/ppermute | solution.py:21
  49.2 2.0 %collective-permute-done.5 = bf16[128,1152]{1,0:T(8,128)(2,1)S(1)} collective-permute-done((bf16[128,1152]{1,0:T(8,128)(2,1)S(1)}, bf16[128,1152]{1,0:T(8,128)(2,1)S(1)}, u32[]{:S(2)}, u32[]{:S(2)}) %collective-permute-start.5) | collective-permute-done | bytes 294944 | tf_op jit(solution)/shard_map/ppermute | solution.py:21
  51.3 3.1 %collective-permute-start.7 = (bf16[128,1152]{1,0:T(8,128)(2,1)S(1)}, bf16[128,1152]{1,0:T(8,128)(2,1)S(1)}, u32[]{:S(2)}, u32[]{:S(2)}) collective-permute-start(bf16[128,1152]{1,0:T(8,128)(2,1)S(1)} %collective-permute-done.5), channel_id=1, source_target_pairs={{0,16},{1,113},{2,18},{3,115},{4,20},{5,117},{6,22},{7,119},{8,24}... | collective-permute-start | bytes 884744 | tf_op jit(solution)/shard_map/ppermute | solution.py:21
  54.5 3.5 %collective-permute-done.7 = bf16[128,1152]{1,0:T(8,128)(2,1)S(1)} collective-permute-done((bf16[128,1152]{1,0:T(8,128)(2,1)S(1)}, bf16[128,1152]{1,0:T(8,128)(2,1)S(1)}, u32[]{:S(2)}, u32[]{:S(2)}) %collective-permute-start.7) | collective-permute-done | bytes 294944 | tf_op jit(solution)/shard_map/ppermute | solution.py:21
  58.1 3.2 %collective-permute-start.9 = (bf16[64,1152]{1,0:T(8,128)(2,1)S(1)}, bf16[64,1152]{1,0:T(8,128)(2,1)S(1)}, u32[]{:S(2)}, u32[]{:S(2)}) collective-permute-start(bf16[64,1152]{1,0:T(8,128)(2,1)S(1)} %slice_select_fusion.2), channel_id=1, source_target_pairs={{0,16},{1,113},{2,18},{3,115},{4,20},{5,117},{6,22},{7,119},{8,24}... | collective-permute-start | bytes 442376 | tf_op jit(solution)/shard_map/ppermute | solution.py:21
  61.3 2.0 %collective-permute-done.9 = bf16[64,1152]{1,0:T(8,128)(2,1)S(1)} collective-permute-done((bf16[64,1152]{1,0:T(8,128)(2,1)S(1)}, bf16[64,1152]{1,0:T(8,128)(2,1)S(1)}, u32[]{:S(2)}, u32[]{:S(2)}) %collective-permute-start.9) | collective-permute-done | bytes 147488 | tf_op jit(solution)/shard_map/ppermute | solution.py:21
  63.4 3.0 %collective-permute-start.10 = (bf16[64,1152]{1,0:T(8,128)(2,1)S(1)}, bf16[64,1152]{1,0:T(8,128)(2,1)S(1)}, u32[]{:S(2)}, u32[]{:S(2)}) collective-permute-start(bf16[64,1152]{1,0:T(8,128)(2,1)S(1)} %collective-permute-done.9), channel_id=1, source_target_pairs={{0,1},{1,0},{2,3},{3,2},{4,5},{5,4},{6,7},{7,6},{8,9},{9,8},{10,11... | collective-permute-start | bytes 442376 | tf_op jit(solution)/shard_map/ppermute | solution.py:21
  66.4 1.0 collective-permute-done.10
  67.4 4.1 %fusion.4 = bf16[1024,1024]{1,0:T(8,128)(2,1)S(1)} fusion(bf16[1024,1152]{1,0:T(8,128)(2,1)S(1)} %fusion.29, bf16[1024,1152]{1,0:T(8,128)(2,1)S(1)} %constant_dynamic-update-slice_fusion.9, f32[]{:T(128)} %bitcast.94, f32[]{:T(128)} %bitcast.18, s32[1024]{0:T(1024)S(1)} %constant_dynamic-update-slice_fusion.18, s32[1024]{0:T(1024)S(1)} %constant_dynamic-update-slice_fusion.17), kind=kOutput, calls=%fused_computation.6 | convolution fusion | flops 2427453440 | bytes 6823944 | tf_op jit(solution)/shard_map/dot_general | solution.py:37
  71.5 2.9 %fusion.52 = (bf16[1024,1152]{1,0:T(8,128)(2,1)S(1)}, f32[1024,1152]{1,0:T(8,128)S(1)}) fusion(bf16[1024,1024]{1,0:T(8,128)(2,1)S(1)} %fusion.4, bf16[1024,1152]{1,0:T(8,128)(2,1)S(1)} %constant_dynamic-update-slice_fusion.9), kind=kOutput, calls=%fused_computation.126 | convolution fusion | flops 2417098752 | bytes 11534336 | tf_op jit(solution)/shard_map/dot_general | solution.py:106
  74.6 0.5 collective-permute-start.17
  75.0 3.0 %fusion.53 = (bf16[1024,1152]{1,0:T(8,128)(2,1)S(1)}, f32[1024,1152]{1,0:T(8,128)S(1)}) fusion(bf16[1024,1024]{1,0:T(8,128)(2,1)S(1)} %fusion.4, bf16[1024,1152]{1,0:T(8,128)(2,1)S(1)} %fusion.29), kind=kOutput, calls=%fused_computation.127 | convolution fusion | flops 2417098752 | bytes 11534336 | tf_op jit(solution)/shard_map/dot_general | solution.py:107
  78.4 2.7 %collective-permute-start.26 = (bf16[128,1152]{1,0:T(8,128)(2,1)S(1)}, bf16[128,1152]{1,0:T(8,128)(2,1)S(1)}, u32[]{:S(2)}, u32[]{:S(2)}) collective-permute-start(bf16[128,1152]{1,0:T(8,128)(2,1)S(1)} %get-tuple-element.19), channel_id=1, source_target_pairs={{0,12},{1,13},{2,14},{3,15},{4,0},{5,1},{6,2},{7,3},{8,4},{9,5},{1... | collective-permute-start | bytes 884744 | tf_op jit(solution)/shard_map/ppermute | solution.py:21
  81.0 0.2 collective-permute-start.29
  81.3 1.2 collective-permute-start.28
  82.5 0.9 collective-permute-done.18
  83.4 0.1 fusion.19
  83.5 0.3 collective-permute-start.19
  83.8 3.4 %collective-permute-done.24 = bf16[128,1152]{1,0:T(8,128)(2,1)S(1)} collective-permute-done((bf16[128,1152]{1,0:T(8,128)(2,1)S(1)}, bf16[128,1152]{1,0:T(8,128)(2,1)S(1)}, u32[]{:S(2)}, u32[]{:S(2)}) %collective-permute-start.24) | collective-permute-done | bytes 294944 | tf_op jit(solution)/shard_map/ppermute | solution.py:21
  87.3 3.5 %collective-permute-done.19 = bf16[128,1152]{1,0:T(8,128)(2,1)S(1)} collective-permute-done((bf16[128,1152]{1,0:T(8,128)(2,1)S(1)}, bf16[128,1152]{1,0:T(8,128)(2,1)S(1)}, u32[]{:S(2)}, u32[]{:S(2)}) %collective-permute-start.19) | collective-permute-done | bytes 294944 | tf_op jit(solution)/shard_map/ppermute | solution.py:21
  90.9 0.1 fusion.21
  91.1 1.4 %collective-permute-done.29 = bf16[128,1152]{1,0:T(8,128)(2,1)S(1)} collective-permute-done((bf16[128,1152]{1,0:T(8,128)(2,1)S(1)}, bf16[128,1152]{1,0:T(8,128)(2,1)S(1)}, u32[]{:S(2)}, u32[]{:S(2)}) %collective-permute-start.29) | collective-permute-done | bytes 294944 | tf_op jit(solution)/shard_map/ppermute | solution.py:21
  92.5 7.3 %collective-permute-done.25 = bf16[128,1152]{1,0:T(8,128)(2,1)S(1)} collective-permute-done((bf16[128,1152]{1,0:T(8,128)(2,1)S(1)}, bf16[128,1152]{1,0:T(8,128)(2,1)S(1)}, u32[]{:S(2)}, u32[]{:S(2)}) %collective-permute-start.25) | collective-permute-done | bytes 294944 | tf_op jit(solution)/shard_map/ppermute | solution.py:21
  99.8 0.2 fusion.33
  100.0 0.3 collective-permute-start.30
  100.3 4.3 %collective-permute-start.27 = (bf16[128,1152]{1,0:T(8,128)(2,1)S(1)}, bf16[128,1152]{1,0:T(8,128)(2,1)S(1)}, u32[]{:S(2)}, u32[]{:S(2)}) collective-permute-start(bf16[128,1152]{1,0:T(8,128)(2,1)S(1)} %get-tuple-element.11), channel_id=1, source_target_pairs={{0,128},{1,129},{2,130},{3,131},{4,132},{5,133},{6,134},{7,135},{8... | collective-permute-start | bytes 884744 | tf_op jit(solution)/shard_map/ppermute | solution.py:21
  104.6 0.1 fusion.23
  104.8 2.0 %collective-permute-done.30 = bf16[128,1152]{1,0:T(8,128)(2,1)S(1)} collective-permute-done((bf16[128,1152]{1,0:T(8,128)(2,1)S(1)}, bf16[128,1152]{1,0:T(8,128)(2,1)S(1)}, u32[]{:S(2)}, u32[]{:S(2)}) %collective-permute-start.30) | collective-permute-done | bytes 294944 | tf_op jit(solution)/shard_map/ppermute | solution.py:21
  106.9 0.1 fusion.15
  107.0 5.5 %collective-permute-start.31 = (bf16[128,1152]{1,0:T(8,128)(2,1)S(1)}, bf16[128,1152]{1,0:T(8,128)(2,1)S(1)}, u32[]{:S(2)}, u32[]{:S(2)}) collective-permute-start(bf16[128,1152]{1,0:T(8,128)(2,1)S(1)} %fusion.15), channel_id=1, source_target_pairs={{0,130},{1,131},{2,128},{3,129},{4,134},{5,135},{6,132},{7,133},{8... | collective-permute-start | bytes 884744 | tf_op jit(solution)/shard_map/ppermute | solution.py:21
  112.4 0.7 collective-permute-start.32
  113.2 1.3 %collective-permute-start.22 = (bf16[128,1152]{1,0:T(8,128)(2,1)S(1)}, bf16[128,1152]{1,0:T(8,128)(2,1)S(1)}, u32[]{:S(2)}, u32[]{:S(2)}) collective-permute-start(bf16[128,1152]{1,0:T(8,128)(2,1)S(1)} %fusion.24), channel_id=1, source_target_pairs={{128,1},{130,3},{132,5},{134,7},{136,9},{138,11},{140,13},{142,15}... | collective-permute-start | bytes 884744 | tf_op jit(solution)/shard_map/ppermute | solution.py:21
  114.5 3.5 %collective-permute-start.23 = (bf16[128,1152]{1,0:T(8,128)(2,1)S(1)}, bf16[128,1152]{1,0:T(8,128)(2,1)S(1)}, u32[]{:S(2)}, u32[]{:S(2)}) collective-permute-start(bf16[128,1152]{1,0:T(8,128)(2,1)S(1)} %fusion.24), channel_id=1, source_target_pairs={{1,0},{3,2},{5,4},{7,6},{9,8},{11,10},{13,12},{15,14},{17,16},{19,... | collective-permute-start | bytes 884744 | tf_op jit(solution)/shard_map/ppermute | solution.py:21
  118.0 5.7 %collective-permute-done.31 = bf16[128,1152]{1,0:T(8,128)(2,1)S(1)} collective-permute-done((bf16[128,1152]{1,0:T(8,128)(2,1)S(1)}, bf16[128,1152]{1,0:T(8,128)(2,1)S(1)}, u32[]{:S(2)}, u32[]{:S(2)}) %collective-permute-start.31) | collective-permute-done | bytes 294944 | tf_op jit(solution)/shard_map/ppermute | solution.py:21
  123.7 4.2 %collective-permute-done.22 = bf16[128,1152]{1,0:T(8,128)(2,1)S(1)} collective-permute-done((bf16[128,1152]{1,0:T(8,128)(2,1)S(1)}, bf16[128,1152]{1,0:T(8,128)(2,1)S(1)}, u32[]{:S(2)}, u32[]{:S(2)}) %collective-permute-start.22) | collective-permute-done | bytes 294944 | tf_op jit(solution)/shard_map/ppermute | solution.py:21
  127.9 1.2 select_bitcast_fusion
  (64 shorter events, 1.5 us)
Async XLA Ops:
  0.0 3.2 %copy-start = (bf16[1,1152,1152]{2,1,0:T(8,128)(2,1)S(1)}, bf16[1,1152,1152]{2,1,0:T(8,128)(2,1)}, u32[]{:S(2)}) copy-start(bf16[1,1152,1152]{2,1,0:T(8,128)(2,1)} %param.8) | copy-start | bytes 7962628
  5.7 19.5 %collective-permute-start.2 = (bf16[128,1152]{1,0:T(8,128)(2,1)}, bf16[128,1152]{1,0:T(8,128)(2,1)S(1)}, u32[]{:S(2)}, u32[]{:S(2)}) collective-permute-start(bf16[128,1152]{1,0:T(8,128)(2,1)} %multiply_convert_fusion), channel_id=1, source_target_pairs={{1,129},{3,131},{5,133},{7,135},{9,137},{11,139},{13,141},{15,143}... | collective-permute-start | bytes 884744 | tf_op jit(solution)/shard_map/ppermute | solution.py:21
  9.6 17.0 %collective-permute-start = (bf16[128,1152]{1,0:T(8,128)(2,1)}, bf16[128,1152]{1,0:T(8,128)(2,1)}, u32[]{:S(2)}, u32[]{:S(2)}) collective-permute-start(bf16[128,1152]{1,0:T(8,128)(2,1)} %multiply_convert_fusion), channel_id=1, source_target_pairs={{0,1},{2,3},{4,5},{6,7},{8,9},{10,11},{12,13},{14,15},{16,17},{18,... | collective-permute-start | bytes 884744 | tf_op jit(solution)/shard_map/ppermute | solution.py:21
  10.9 15.7 %collective-permute-start.1 = (bf16[128,1152]{1,0:T(8,128)(2,1)}, bf16[128,1152]{1,0:T(8,128)(2,1)}, u32[]{:S(2)}, u32[]{:S(2)}) collective-permute-start(bf16[128,1152]{1,0:T(8,128)(2,1)} %multiply_convert_fusion), channel_id=1, source_target_pairs={{1,128},{3,130},{5,132},{7,134},{9,136},{11,138},{13,140},{15,142}... | collective-permute-start | bytes 884744 | tf_op jit(solution)/shard_map/ppermute | solution.py:21
  25.3 11.3 %collective-permute-start.11 = (bf16[128,1152]{1,0:T(8,128)(2,1)S(1)}, bf16[128,1152]{1,0:T(8,128)(2,1)S(1)}, u32[]{:S(2)}, u32[]{:S(2)}) collective-permute-start(bf16[128,1152]{1,0:T(8,128)(2,1)S(1)} %get-tuple-element.8), channel_id=1, source_target_pairs={{0,4},{1,5},{2,6},{3,7},{4,8},{5,9},{6,10},{7,11},{8,12},{9,13},{1... | collective-permute-start | bytes 884744 | tf_op jit(solution)/shard_map/ppermute | solution.py:21
  28.0 14.0 %collective-permute-start.12 = (bf16[128,1152]{1,0:T(8,128)(2,1)S(1)}, bf16[128,1152]{1,0:T(8,128)(2,1)S(1)}, u32[]{:S(2)}, u32[]{:S(2)}) collective-permute-start(bf16[128,1152]{1,0:T(8,128)(2,1)S(1)} %get-tuple-element.6), channel_id=1, source_target_pairs={{0,4},{1,5},{2,6},{3,7},{4,8},{5,9},{6,10},{7,11},{8,12},{9,13},{1... | collective-permute-start | bytes 884744 | tf_op jit(solution)/shard_map/ppermute | solution.py:21
  29.4 18.2 %collective-permute-start.14 = (bf16[128,1152]{1,0:T(8,128)(2,1)S(1)}, bf16[128,1152]{1,0:T(8,128)(2,1)S(1)}, u32[]{:S(2)}, u32[]{:S(2)}) collective-permute-start(bf16[128,1152]{1,0:T(8,128)(2,1)S(1)} %get-tuple-element.6), channel_id=1, source_target_pairs={{0,12},{1,13},{2,14},{3,15},{4,0},{5,1},{6,2},{7,3},{8,4},{9,5},{1... | collective-permute-start | bytes 884744 | tf_op jit(solution)/shard_map/ppermute | solution.py:21
  30.8 9.2 %collective-permute-start.3 = (bf16[128,1152]{1,0:T(8,128)(2,1)S(1)}, bf16[128,1152]{1,0:T(8,128)(2,1)S(1)}, u32[]{:S(2)}, u32[]{:S(2)}) collective-permute-start(bf16[128,1152]{1,0:T(8,128)(2,1)S(1)} %get-tuple-element.21), channel_id=1, source_target_pairs={{0,16},{1,113},{2,18},{3,115},{4,20},{5,117},{6,22},{7,119},{8,24}... | collective-permute-start | bytes 884744 | tf_op jit(solution)/shard_map/ppermute | solution.py:21
  36.3 12.7 %collective-permute-start.13 = (bf16[128,1152]{1,0:T(8,128)(2,1)S(1)}, bf16[128,1152]{1,0:T(8,128)(2,1)S(1)}, u32[]{:S(2)}, u32[]{:S(2)}) collective-permute-start(bf16[128,1152]{1,0:T(8,128)(2,1)S(1)} %get-tuple-element.8), channel_id=1, source_target_pairs={{0,12},{1,13},{2,14},{3,15},{4,0},{5,1},{6,2},{7,3},{8,4},{9,5},{1... | collective-permute-start | bytes 884744 | tf_op jit(solution)/shard_map/ppermute | solution.py:21
  36.7 17.8 %collective-permute-start.15 = (bf16[128,1152]{1,0:T(8,128)(2,1)S(1)}, bf16[128,1152]{1,0:T(8,128)(2,1)S(1)}, u32[]{:S(2)}, u32[]{:S(2)}) collective-permute-start(bf16[128,1152]{1,0:T(8,128)(2,1)S(1)} %collective-permute-done.11), channel_id=1, source_target_pairs={{0,4},{1,5},{2,6},{3,7},{4,8},{5,9},{6,10},{7,11},{8,12},{9,13},{1... | collective-permute-start | bytes 884744 | tf_op jit(solution)/shard_map/ppermute | solution.py:21
  40.0 14.4 %collective-permute-start.4 = (bf16[128,1152]{1,0:T(8,128)(2,1)S(1)}, bf16[128,1152]{1,0:T(8,128)(2,1)S(1)}, u32[]{:S(2)}, u32[]{:S(2)}) collective-permute-start(bf16[128,1152]{1,0:T(8,128)(2,1)S(1)} %collective-permute-done.3), channel_id=1, source_target_pairs={{0,1},{1,0},{2,3},{3,2},{4,5},{5,4},{6,7},{7,6},{8,9},{9,8},{10,11... | collective-permute-start | bytes 884744 | tf_op jit(solution)/shard_map/ppermute | solution.py:21
  42.0 9.2 %collective-permute-start.5 = (bf16[128,1152]{1,0:T(8,128)(2,1)S(1)}, bf16[128,1152]{1,0:T(8,128)(2,1)S(1)}, u32[]{:S(2)}, u32[]{:S(2)}) collective-permute-start(bf16[128,1152]{1,0:T(8,128)(2,1)S(1)} %collective-permute-done.3), channel_id=1, source_target_pairs={{0,16},{1,113},{2,18},{3,115},{4,20},{5,117},{6,22},{7,119},{8,24}... | collective-permute-start | bytes 884744 | tf_op jit(solution)/shard_map/ppermute | solution.py:21
  47.6 6.9 %collective-permute-start.16 = (bf16[128,1152]{1,0:T(8,128)(2,1)S(1)}, bf16[128,1152]{1,0:T(8,128)(2,1)S(1)}, u32[]{:S(2)}, u32[]{:S(2)}) collective-permute-start(bf16[128,1152]{1,0:T(8,128)(2,1)S(1)} %collective-permute-done.14), channel_id=1, source_target_pairs={{0,12},{1,13},{2,14},{3,15},{4,0},{5,1},{6,2},{7,3},{8,4},{9,5},{1... | collective-permute-start | bytes 884744 | tf_op jit(solution)/shard_map/ppermute | solution.py:21
  51.3 10.0 %collective-permute-start.6 = (bf16[128,1152]{1,0:T(8,128)(2,1)S(1)}, bf16[128,1152]{1,0:T(8,128)(2,1)S(1)}, u32[]{:S(2)}, u32[]{:S(2)}) collective-permute-start(bf16[128,1152]{1,0:T(8,128)(2,1)S(1)} %collective-permute-done.5), channel_id=1, source_target_pairs={{0,1},{1,0},{2,3},{3,2},{4,5},{5,4},{6,7},{7,6},{8,9},{9,8},{10,11... | collective-permute-start | bytes 884744 | tf_op jit(solution)/shard_map/ppermute | solution.py:21
  51.3 6.8 %collective-permute-start.7 = (bf16[128,1152]{1,0:T(8,128)(2,1)S(1)}, bf16[128,1152]{1,0:T(8,128)(2,1)S(1)}, u32[]{:S(2)}, u32[]{:S(2)}) collective-permute-start(bf16[128,1152]{1,0:T(8,128)(2,1)S(1)} %collective-permute-done.5), channel_id=1, source_target_pairs={{0,16},{1,113},{2,18},{3,115},{4,20},{5,117},{6,22},{7,119},{8,24}... | collective-permute-start | bytes 884744 | tf_op jit(solution)/shard_map/ppermute | solution.py:21
  58.1 5.3 %collective-permute-start.9 = (bf16[64,1152]{1,0:T(8,128)(2,1)S(1)}, bf16[64,1152]{1,0:T(8,128)(2,1)S(1)}, u32[]{:S(2)}, u32[]{:S(2)}) collective-permute-start(bf16[64,1152]{1,0:T(8,128)(2,1)S(1)} %slice_select_fusion.2), channel_id=1, source_target_pairs={{0,16},{1,113},{2,18},{3,115},{4,20},{5,117},{6,22},{7,119},{8,24}... | collective-permute-start | bytes 442376 | tf_op jit(solution)/shard_map/ppermute | solution.py:21
  61.3 5.1 %collective-permute-start.8 = (bf16[128,1152]{1,0:T(8,128)(2,1)S(1)}, bf16[128,1152]{1,0:T(8,128)(2,1)S(1)}, u32[]{:S(2)}, u32[]{:S(2)}) collective-permute-start(bf16[128,1152]{1,0:T(8,128)(2,1)S(1)} %collective-permute-done.7), channel_id=1, source_target_pairs={{0,1},{1,0},{2,3},{3,2},{4,5},{5,4},{6,7},{7,6},{8,9},{9,8},{10,11... | collective-permute-start | bytes 884744 | tf_op jit(solution)/shard_map/ppermute | solution.py:21
  63.4 4.0 %collective-permute-start.10 = (bf16[64,1152]{1,0:T(8,128)(2,1)S(1)}, bf16[64,1152]{1,0:T(8,128)(2,1)S(1)}, u32[]{:S(2)}, u32[]{:S(2)}) collective-permute-start(bf16[64,1152]{1,0:T(8,128)(2,1)S(1)} %collective-permute-done.9), channel_id=1, source_target_pairs={{0,1},{1,0},{2,3},{3,2},{4,5},{5,4},{6,7},{7,6},{8,9},{9,8},{10,11... | collective-permute-start | bytes 442376 | tf_op jit(solution)/shard_map/ppermute | solution.py:21
  74.6 3.4 %collective-permute-start.17 = (bf16[448,1152]{1,0:T(8,128)(2,1)S(1)}, bf16[448,1152]{1,0:T(8,128)(2,1)S(1)}, u32[]{:S(2)}, u32[]{:S(2)}) collective-permute-start(bf16[448,1152]{1,0:T(8,128)(2,1)S(1)} %pad_maximum_fusion), channel_id=1, source_target_pairs={{0,1},{1,0},{2,3},{3,2},{4,5},{5,4},{6,7},{7,6},{8,9},{9,8},{10,11... | collective-permute-start | bytes 3096584 | tf_op jit(solution)/shard_map/ppermute | solution.py:21
  78.1 5.3 %collective-permute-start.18 = (bf16[64,1152]{1,0:T(8,128)(2,1)S(1)}, bf16[64,1152]{1,0:T(8,128)(2,1)S(1)}, u32[]{:S(2)}, u32[]{:S(2)}) collective-permute-start(bf16[64,1152]{1,0:T(8,128)(2,1)S(1)} %fusion.28), channel_id=1, source_target_pairs={{0,112},{1,17},{2,114},{3,19},{4,116},{5,21},{6,118},{7,23},{8,120... | collective-permute-start | bytes 442376 | tf_op jit(solution)/shard_map/ppermute | solution.py:21
  78.3 8.9 %collective-permute-start.24 = (bf16[128,1152]{1,0:T(8,128)(2,1)S(1)}, bf16[128,1152]{1,0:T(8,128)(2,1)S(1)}, u32[]{:S(2)}, u32[]{:S(2)}) collective-permute-start(bf16[128,1152]{1,0:T(8,128)(2,1)S(1)} %get-tuple-element.16), channel_id=1, source_target_pairs={{0,4},{1,5},{2,6},{3,7},{4,8},{5,9},{6,10},{7,11},{8,12},{9,13},{1... | collective-permute-start | bytes 884744 | tf_op jit(solution)/shard_map/ppermute | solution.py:21
  78.4 12.7 %collective-permute-start.26 = (bf16[128,1152]{1,0:T(8,128)(2,1)S(1)}, bf16[128,1152]{1,0:T(8,128)(2,1)S(1)}, u32[]{:S(2)}, u32[]{:S(2)}) collective-permute-start(bf16[128,1152]{1,0:T(8,128)(2,1)S(1)} %get-tuple-element.19), channel_id=1, source_target_pairs={{0,12},{1,13},{2,14},{3,15},{4,0},{5,1},{6,2},{7,3},{8,4},{9,5},{1... | collective-permute-start | bytes 884744 | tf_op jit(solution)/shard_map/ppermute | solution.py:21
  81.0 11.5 %collective-permute-start.29 = (bf16[128,1152]{1,0:T(8,128)(2,1)S(1)}, bf16[128,1152]{1,0:T(8,128)(2,1)S(1)}, u32[]{:S(2)}, u32[]{:S(2)}) collective-permute-start(bf16[128,1152]{1,0:T(8,128)(2,1)S(1)} %get-tuple-element.17), channel_id=1, source_target_pairs={{0,12},{1,13},{2,14},{3,15},{4,0},{5,1},{6,2},{7,3},{8,4},{9,5},{1... | collective-permute-start | bytes 884744 | tf_op jit(solution)/shard_map/ppermute | solution.py:21
  81.3 23.6 %collective-permute-start.28 = (bf16[128,1152]{1,0:T(8,128)(2,1)S(1)}, bf16[128,1152]{1,0:T(8,128)(2,1)S(1)}, u32[]{:S(2)}, u32[]{:S(2)}) collective-permute-start(bf16[128,1152]{1,0:T(8,128)(2,1)S(1)} %get-tuple-element.18), channel_id=1, source_target_pairs={{0,4},{1,5},{2,6},{3,7},{4,8},{5,9},{6,10},{7,11},{8,12},{9,13},{1... | collective-permute-start | bytes 884744 | tf_op jit(solution)/shard_map/ppermute | solution.py:21
  83.5 7.4 %collective-permute-start.19 = (bf16[128,1152]{1,0:T(8,128)(2,1)S(1)}, bf16[128,1152]{1,0:T(8,128)(2,1)S(1)}, u32[]{:S(2)}, u32[]{:S(2)}) collective-permute-start(bf16[128,1152]{1,0:T(8,128)(2,1)S(1)} %fusion.19), channel_id=1, source_target_pairs={{0,112},{1,17},{2,114},{3,19},{4,116},{5,21},{6,118},{7,23},{8,120... | collective-permute-start | bytes 884744 | tf_op jit(solution)/shard_map/ppermute | solution.py:21
  87.3 12.6 %collective-permute-start.25 = (bf16[128,1152]{1,0:T(8,128)(2,1)S(1)}, bf16[128,1152]{1,0:T(8,128)(2,1)S(1)}, u32[]{:S(2)}, u32[]{:S(2)}) collective-permute-start(bf16[128,1152]{1,0:T(8,128)(2,1)S(1)} %fusion.16), channel_id=1, source_target_pairs={{0,4},{1,5},{2,6},{3,7},{4,8},{5,9},{6,10},{7,11},{8,12},{9,13},{1... | collective-permute-start | bytes 884744 | tf_op jit(solution)/shard_map/ppermute | solution.py:21
  91.0 13.6 %collective-permute-start.20 = (bf16[128,1152]{1,0:T(8,128)(2,1)S(1)}, bf16[128,1152]{1,0:T(8,128)(2,1)S(1)}, u32[]{:S(2)}, u32[]{:S(2)}) collective-permute-start(bf16[128,1152]{1,0:T(8,128)(2,1)S(1)} %fusion.21), channel_id=1, source_target_pairs={{0,112},{1,17},{2,114},{3,19},{4,116},{5,21},{6,118},{7,23},{8,120... | collective-permute-start | bytes 884744 | tf_op jit(solution)/shard_map/ppermute | solution.py:21
  100.0 6.9 %collective-permute-start.30 = (bf16[128,1152]{1,0:T(8,128)(2,1)S(1)}, bf16[128,1152]{1,0:T(8,128)(2,1)S(1)}, u32[]{:S(2)}, u32[]{:S(2)}) collective-permute-start(bf16[128,1152]{1,0:T(8,128)(2,1)S(1)} %get-tuple-element.12), channel_id=1, source_target_pairs={{0,12},{1,13},{2,14},{3,15},{4,0},{5,1},{6,2},{7,3},{8,4},{9,5},{1... | collective-permute-start | bytes 884744 | tf_op jit(solution)/shard_map/ppermute | solution.py:21
  100.3 17.7 %collective-permute-start.27 = (bf16[128,1152]{1,0:T(8,128)(2,1)S(1)}, bf16[128,1152]{1,0:T(8,128)(2,1)S(1)}, u32[]{:S(2)}, u32[]{:S(2)}) collective-permute-start(bf16[128,1152]{1,0:T(8,128)(2,1)S(1)} %get-tuple-element.11), channel_id=1, source_target_pairs={{0,128},{1,129},{2,130},{3,131},{4,132},{5,133},{6,134},{7,135},{8... | collective-permute-start | bytes 884744 | tf_op jit(solution)/shard_map/ppermute | solution.py:21
  104.7 8.4 %collective-permute-start.21 = (bf16[128,1152]{1,0:T(8,128)(2,1)S(1)}, bf16[128,1152]{1,0:T(8,128)(2,1)S(1)}, u32[]{:S(2)}, u32[]{:S(2)}) collective-permute-start(bf16[128,1152]{1,0:T(8,128)(2,1)S(1)} %fusion.23), channel_id=1, source_target_pairs={{0,112},{1,17},{2,114},{3,19},{4,116},{5,21},{6,118},{7,23},{8,120... | collective-permute-start | bytes 884744 | tf_op jit(solution)/shard_map/ppermute | solution.py:21
  107.0 16.7 %collective-permute-start.31 = (bf16[128,1152]{1,0:T(8,128)(2,1)S(1)}, bf16[128,1152]{1,0:T(8,128)(2,1)S(1)}, u32[]{:S(2)}, u32[]{:S(2)}) collective-permute-start(bf16[128,1152]{1,0:T(8,128)(2,1)S(1)} %fusion.15), channel_id=1, source_target_pairs={{0,130},{1,131},{2,128},{3,129},{4,134},{5,135},{6,132},{7,133},{8... | collective-permute-start | bytes 884744 | tf_op jit(solution)/shard_map/ppermute | solution.py:21
  112.4 11.3 %collective-permute-start.32 = (bf16[128,1152]{1,0:T(8,128)(2,1)S(1)}, bf16[128,1152]{1,0:T(8,128)(2,1)S(1)}, u32[]{:S(2)}, u32[]{:S(2)}) collective-permute-start(bf16[128,1152]{1,0:T(8,128)(2,1)S(1)} %fusion.15), channel_id=1, source_target_pairs={{128,130},{129,131},{130,128},{131,129},{132,134},{133,135},{134,1... | collective-permute-start | bytes 884744 | tf_op jit(solution)/shard_map/ppermute | solution.py:21
  113.2 14.7 %collective-permute-start.22 = (bf16[128,1152]{1,0:T(8,128)(2,1)S(1)}, bf16[128,1152]{1,0:T(8,128)(2,1)S(1)}, u32[]{:S(2)}, u32[]{:S(2)}) collective-permute-start(bf16[128,1152]{1,0:T(8,128)(2,1)S(1)} %fusion.24), channel_id=1, source_target_pairs={{128,1},{130,3},{132,5},{134,7},{136,9},{138,11},{140,13},{142,15}... | collective-permute-start | bytes 884744 | tf_op jit(solution)/shard_map/ppermute | solution.py:21
  114.5 13.4 %collective-permute-start.23 = (bf16[128,1152]{1,0:T(8,128)(2,1)S(1)}, bf16[128,1152]{1,0:T(8,128)(2,1)S(1)}, u32[]{:S(2)}, u32[]{:S(2)}) collective-permute-start(bf16[128,1152]{1,0:T(8,128)(2,1)S(1)} %fusion.24), channel_id=1, source_target_pairs={{1,0},{3,2},{5,4},{7,6},{9,8},{11,10},{13,12},{15,14},{17,16},{19,... | collective-permute-start | bytes 884744 | tf_op jit(solution)/shard_map/ppermute | solution.py:21
